TPU v7x, 512 devices: a 8x2x16 block of a 8x8x16 slice. The times are simulated.
512 devices in a mesh: runs: 2 (over y), gx: 16 (over z), gy: 8 (over x), gz: 2 (over core).
Axes of the slice: x: 8, y: 2, z: 16, core: 2. Of those that a mesh axis runs over, the one named last changes fastest.
The devices are a block of a 8x8x16 slice.
Arguments:
- positions: float32 [3, 8, 65536], P(None, None, ('runs', 'gx', 'gy', 'gz')), parts along dimension 2, as said below
- velocities: float32 [3, 8, 65536], P(None, None, ('runs', 'gx', 'gy', 'gz')), parts along dimension 2, may hold values from -5 to 5
- send_list: int32 [91136], P(('runs', 'gx', 'gy', 'gz')), parts along dimension 0, may hold values from 0 to 127
- pair_list: int32 [2, 917504], P(None, ('runs', 'gx', 'gy', 'gz')), parts along dimension 1, may hold values from 0 to 306, as said below
- constraint_flags: int32 [7, 65536], P(None, ('runs', 'gx', 'gy', 'gz')), parts along dimension 1, may hold values 0 or 1
Outputs:
- final_positions: float32 [3, 8, 65536], P(None, None, ('runs', 'gx', 'gy', 'gz')), parts along dimension 2
- final_velocities: float32 [3, 8, 65536], P(None, None, ('runs', 'gx', 'gy', 'gz')), parts along dimension 2
- energies: float32 [6, 2], P('runs'), parts along dimension 0
There are 2 independent parts, one for each index of `runs`. A program takes and returns all parts, laid end to end along the dimension named above; each array names one. Nothing has to cross between parts.
Inputs may be any that keep to these rules, and one draw needn't show every extreme that they name: `pair_list`: each domain's 1792 slots name clusters of its extended set: 0 to 127 its own, then its received zone blocks in order; padding slots hold 306 in both rows; every cluster appears in a slot with itself; no unordered pair appears twice. `positions`: eight beads of a cluster lie in its cell of side 1, the cells of a domain filling a box of 1 by 8 by 16; neighbouring beads of a cluster are between 0.25 and 0.6 apart.
All inputs are finite; a program needn't handle non-finite values. No bound on the sum of `constraint_flags` on one device may be relied on, other than what follows from the above.
Results may differ from a plain program's by a relative error of at most 0.0003.
Values sent between devices are 32-bit elements; how exact they have to be, the bound alone decides.
A program may use at most 64 MiB of HBM per device.

v0:
```python
import jax
import jax.numpy as jnp
import numpy as np
from jax import lax
from jax.sharding import PartitionSpec as P

CX = 1
CY = 8
CZ = 16
ITERS = 3
NORDER = 4
time_step = 0.02
strength = 2.0
root_half = 0.7071067811865476
zone_list = ((1, 0, 0), (0, 1, 0), (0, 0, 1), (1, 1, 0), (1, 0, 1), (0, 1, 1), (1, 1, 1))


def from_behind(value, axis, by):
    count = lax.axis_size(axis)
    return lax.ppermute(value, axis, [(i, (i + by) % count) for i in range(count)])


def over_axes(value, axes):
    for axis in axes:
        value = lax.psum(value, axis)
    return value


def zone_sizes():
    return tuple(
        (
            (CX if direction[0] == 0 else 1)
            * (CY if direction[1] == 0 else 1)
            * (CZ if direction[2] == 0 else 1)
            for direction in zone_list
        )
    )


def split_blocks(packed, block_sizes):
    pieces = []
    position = 0
    for length in block_sizes:
        pieces.append(packed[:, :, position : position + length])
        position += length
    return pieces


def shell_offsets():
    block_sizes = zone_sizes()
    columns = []
    for number in range(7):
        direction = zone_list[number]
        column = np.array(
            [[direction[0] * CX], [direction[1] * CY], [direction[2] * CZ]], np.float32
        )
        columns.append(np.tile(column, (1, block_sizes[number])))
    return jnp.asarray(np.concatenate(columns, axis=1))[:, None, :]


def share_coords(coords, send_list):
    sizes_all = zone_sizes()
    outgoing = split_blocks(jnp.take(coords, send_list, axis=2), sizes_all)
    along_y = from_behind(
        jnp.concatenate([outgoing[1], outgoing[3], outgoing[5], outgoing[6]], axis=2), "gy", -1
    )
    got_y = split_blocks(along_y, [sizes_all[1], sizes_all[3], sizes_all[5], sizes_all[6]])
    along_x = from_behind(
        jnp.concatenate([outgoing[0], outgoing[4], got_y[1], got_y[3]], axis=2), "gx", -1
    )
    got_x = split_blocks(along_x, [sizes_all[0], sizes_all[4], sizes_all[3], sizes_all[6]])
    along_z = from_behind(
        jnp.concatenate([outgoing[2], got_x[1], got_y[2], got_x[3]], axis=2), "gz", -1
    )
    got_z = split_blocks(along_z, [sizes_all[2], sizes_all[4], sizes_all[5], sizes_all[6]])
    received = [got_x[0], got_y[0], got_z[0], got_x[2], got_z[1], got_z[2], got_z[3]]
    return jnp.concatenate(received, axis=2) + shell_offsets()


def return_forces(halo_forces):
    sizes_all = zone_sizes()
    outgoing = split_blocks(halo_forces, sizes_all)
    along_z = from_behind(
        jnp.concatenate([outgoing[2], outgoing[4], outgoing[5], outgoing[6]], axis=2), "gz", 1
    )
    got_z = split_blocks(along_z, [sizes_all[2], sizes_all[4], sizes_all[5], sizes_all[6]])
    along_x = from_behind(
        jnp.concatenate([outgoing[0], outgoing[3], got_z[1], got_z[3]], axis=2), "gx", 1
    )
    got_x = split_blocks(along_x, [sizes_all[0], sizes_all[3], sizes_all[4], sizes_all[6]])
    settled = [got_x[0], got_z[0], got_x[2]]
    pending = [got_x[1], got_z[2], got_x[3]]
    along_y = from_behind(
        jnp.concatenate([outgoing[1], pending[0], pending[1], pending[2]], axis=2), "gy", 1
    )
    got_y = split_blocks(along_y, [sizes_all[1], sizes_all[3], sizes_all[5], sizes_all[6]])
    return jnp.concatenate(
        [settled[0], got_y[0], settled[1], got_y[1], settled[2], got_y[2], got_y[3]], axis=2
    )


def pair_tables(pair_list, extended_count):
    rows = lax.broadcasted_iota(jnp.int32, (extended_count, pair_list.shape[1]), 0)
    first_table = (rows == pair_list[0][None, :]).astype(jnp.float32)
    second_table = (rows == pair_list[1][None, :]).astype(jnp.float32)
    return (first_table, second_table)


def domain_forces(extended, pair_list, tables):
    extended_count = extended.shape[2]
    slot_count = pair_list.shape[1]
    first_ids = pair_list[0]
    second_ids = pair_list[1]
    flat = extended.reshape(24, extended_count)
    first_coords = jnp.dot(flat, tables[0], precision=lax.Precision.HIGHEST).reshape(
        3, 8, slot_count
    )
    second_coords = jnp.dot(flat, tables[1], precision=lax.Precision.HIGHEST).reshape(
        3, 8, slot_count
    )
    separation = first_coords[:, :, None, :] - second_coords[:, None, :, :]
    scaled = jnp.sum(separation * separation, axis=0)
    intersect = jnp.maximum(1.0 - scaled, 0.0)
    bead_row = lax.broadcasted_iota(jnp.int32, (8, 8, 1), 0)
    bead_column = lax.broadcasted_iota(jnp.int32, (8, 8, 1), 1)
    self_pair = (first_ids == second_ids)[None, None, :]
    usable = (first_ids < extended_count - 1)[None, None, :]
    weight = (jnp.where(self_pair, bead_row < bead_column, True) & usable).astype(jnp.float32)
    energy = strength * jnp.sum(weight * intersect * intersect * intersect)
    magnitude = 6.0 * strength * weight * intersect * intersect
    pushing = magnitude[None] * separation
    on_first = jnp.sum(pushing, axis=2).reshape(24, slot_count)
    on_second = (-jnp.sum(pushing, axis=1)).reshape(24, slot_count)
    contract = (((1,), (1,)), ((), ()))
    forces = lax.dot_general(on_first, tables[0], contract, precision=lax.Precision.HIGHEST)
    forces = forces + lax.dot_general(
        on_second, tables[1], contract, precision=lax.Precision.HIGHEST
    )
    return (forces.reshape(3, 8, extended_count), energy)


def local_forces(coords, send_list, pair_list, tables):
    halo_coords = share_coords(coords, send_list)
    dummy_cluster = jnp.zeros((3, 8, 1), jnp.float32)
    extended = jnp.concatenate([coords, halo_coords, dummy_cluster], axis=2)
    forces, energy = domain_forces(extended, pair_list, tables)
    cluster_count = coords.shape[2]
    returned = return_forces(forces[:, :, cluster_count : cluster_count + send_list.shape[0]])
    home_forces = forces[:, :, :cluster_count].at[:, :, send_list].add(returned)
    return (home_forces, energy)


def link_vectors(coords):
    return coords[:, :-1, :] - coords[:, 1:, :]


def link_lengths(coords):
    vectors = link_vectors(coords)
    return jnp.sqrt(jnp.sum(vectors * vectors, axis=0))


def expand(coupling, source):
    coupling_down = jnp.pad(coupling, ((1, 0), (0, 0)))
    coupling_up = jnp.pad(coupling, ((0, 1), (0, 0)))
    series = source
    result = source
    for expansion in range(NORDER):
        series = (
            coupling_down * jnp.pad(series, ((1, 0), (0, 0)))[:-1]
            + coupling_up * jnp.pad(series, ((0, 1), (0, 0)))[1:]
        )
        result = result + series
    return result


def apply_links(coords, directions, solution):
    shifts = directions * (root_half * solution)[None]
    return (
        coords
        - jnp.pad(shifts, ((0, 0), (0, 1), (0, 0)))
        + jnp.pad(shifts, ((0, 0), (1, 0), (0, 0)))
    )


def constrain(previous, updated, rest_length, link_flags):
    old_vectors = link_vectors(previous)
    directions = (
        old_vectors / jnp.maximum(jnp.sqrt(jnp.sum(old_vectors * old_vectors, axis=0)), 0.2)[None]
    )
    coupling = (
        0.5
        * jnp.sum(directions[:, :-1] * directions[:, 1:], axis=0)
        * link_flags[:-1]
        * link_flags[1:]
    )
    projected = jnp.sum(directions * link_vectors(updated), axis=0)
    solution = expand(coupling, link_flags * root_half * (projected - rest_length))
    updated = apply_links(updated, directions, solution)
    vectors = link_vectors(updated)
    squared = jnp.sum(vectors * vectors, axis=0)
    target = jnp.sqrt(
        jnp.maximum(2.0 * rest_length * rest_length - squared, 0.25 * rest_length * rest_length)
    )
    solution = expand(coupling, link_flags * root_half * (rest_length - target))
    updated = apply_links(updated, directions, solution)
    return updated


def on_device(positions, velocities, send_list, pair_list, constraint_flags):
    link_flags = constraint_flags.astype(jnp.float32)
    rest_length = link_lengths(positions)
    bead_total = 8 * positions.shape[2] * lax.axis_size(("gx", "gy", "gz"))
    tables = pair_tables(pair_list, positions.shape[2] + send_list.shape[0] + 1)
    forces, potential = local_forces(positions, send_list, pair_list, tables)
    energy_rows = []
    for iteration in range(ITERS):
        half_speed = velocities + 0.5 * time_step * forces
        updated = constrain(positions, positions + time_step * half_speed, rest_length, link_flags)
        half_speed = (updated - positions) / time_step
        forces, potential = local_forces(updated, send_list, pair_list, tables)
        velocities = half_speed + 0.5 * time_step * forces
        positions = updated
        kinetic = 0.5 * jnp.sum(velocities * velocities)
        energy_rows.append(jnp.stack([potential, kinetic]))
    energies = jnp.stack(energy_rows)
    energies = over_axes(energies, ("gx", "gy", "gz"))
    return (positions, velocities, energies / bead_total)


def solution(mesh):
    return jax.shard_map(
        on_device,
        mesh=mesh,
        in_specs=(
            P(None, None, ("runs", "gx", "gy", "gz")),
            P(None, None, ("runs", "gx", "gy", "gz")),
            P(("runs", "gx", "gy", "gz")),
            P(None, ("runs", "gx", "gy", "gz")),
            P(None, ("runs", "gx", "gy", "gz")),
        ),
        out_specs=(
            P(None, None, ("runs", "gx", "gy", "gz")),
            P(None, None, ("runs", "gx", "gy", "gz")),
            P("runs", None),
        ),
        check_vma=False,
    )
```

profile of v0, /device:TPU:65, one launch (start us, length us, event | category | flops | bytes accessed | tf_op | source)
XLA Modules:
  0.0 284.2 jit_solution(5822474635701368043)
XLA Ops:
  4.1 6.3 %collective-permute-start = (f32[3,8,34]{2,1,0:T(8,128)S(1)}, f32[3,8,34]{2,1,0:T(8,128)S(1)}, u32[]{:S(2)}, u32[]{:S(2)}) collective-permute-start(f32[3,8,34]{2,1,0:T(8,128)S(1)} %pad_maximum_fusion.8), channel_id=1, source_target_pairs={{0,14},{2,0},{4,2},{6,4},{8,6},{10,8},{12,10},{14,12},{1,15},{3,1}... | collective-permute-start | bytes 9800 | tf_op jit(solution)/shard_map/ppermute | solution.py:20
  11.5 43.7 %collective-permute-start.1 = (f32[3,8,153]{2,1,0:T(8,128)S(1)}, f32[3,8,153]{2,1,0:T(8,128)S(1)}, u32[]{:S(2)}, u32[]{:S(2)}) collective-permute-start(f32[3,8,153]{2,1,0:T(8,128)S(1)} %pad_maximum_fusion), channel_id=1, source_target_pairs={{0,240},{16,0},{32,16},{48,32},{64,48},{80,64},{96,80},{112,96},{1... | collective-permute-start | bytes 44072 | tf_op jit(solution)/shard_map/ppermute | solution.py:20
  56.3 4.2 %collective-permute-start.2 = (f32[3,8,18]{2,1,0:T(8,128)S(1)}, f32[3,8,18]{2,1,0:T(8,128)S(1)}, u32[]{:S(2)}, u32[]{:S(2)}) collective-permute-start(f32[3,8,18]{2,1,0:T(8,128)S(1)} %pad_maximum_fusion.9), channel_id=1, source_target_pairs={{0,1},{1,0},{2,3},{3,2},{4,5},{5,4},{6,7},{7,6},{8,9},{9,8},{10,11... | collective-permute-start | bytes 5192 | tf_op jit(solution)/shard_map/ppermute | solution.py:20
  65.2 1.1 fusion.55
  66.6 2.3 collective-permute-start.3
  69.9 1.9 collective-permute-start.4
  71.9 4.4 %collective-permute-done.4 = f32[3,8,153]{2,1,0:T(8,128)S(1)} collective-permute-done((f32[3,8,153]{2,1,0:T(8,128)S(1)}, f32[3,8,153]{2,1,0:T(8,128)S(1)}, u32[]{:S(2)}, u32[]{:S(2)}) %collective-permute-start.4) | collective-permute-done | bytes 14720 | tf_op jit(solution)/shard_map/ppermute | solution.py:20
  76.5 1.9 collective-permute-start.5
  78.7 4.0 %collective-permute-done.5 = f32[3,8,34]{2,1,0:T(8,128)S(1)} collective-permute-done((f32[3,8,34]{2,1,0:T(8,128)S(1)}, f32[3,8,34]{2,1,0:T(8,128)S(1)}, u32[]{:S(2)}, u32[]{:S(2)}) %collective-permute-start.5) | collective-permute-done | bytes 3296 | tf_op jit(solution)/shard_map/ppermute | solution.py:20
  83.2 7.2 %scatter_fusion = f32[3,8,128]{1,0,2:T(4,128)S(1)} fusion(f32[3,8,128]{1,0,2:T(4,128)S(1)} %copy.120, s32[178]{0:T(256)S(1)} %compare_select_fusion, f32[178,3,8]{2,1,0:T(4,128)S(1)} %copy.102), kind=kCustom, calls=%fused_computation.4 | custom fusion | flops 4272 | bytes 51976 | tf_op jit(solution)/shard_map/scatter-add | solution.py:149
  92.1 3.4 %collective-permute-start.6 = (f32[3,8,34]{2,1,0:T(8,128)S(1)}, f32[3,8,34]{2,1,0:T(8,128)S(1)}, u32[]{:S(2)}, u32[]{:S(2)}) collective-permute-start(f32[3,8,34]{2,1,0:T(8,128)S(1)} %pad_maximum_fusion.12), channel_id=1, source_target_pairs={{0,14},{2,0},{4,2},{6,4},{8,6},{10,8},{12,10},{14,12},{1,15},{3,1}... | collective-permute-start | bytes 9800 | tf_op jit(solution)/shard_map/ppermute | solution.py:20
  96.8 3.4 %collective-permute-start.7 = (f32[3,8,153]{2,1,0:T(8,128)S(1)}, f32[3,8,153]{2,1,0:T(8,128)S(1)}, u32[]{:S(2)}, u32[]{:S(2)}) collective-permute-start(f32[3,8,153]{2,1,0:T(8,128)S(1)} %pad_maximum_fusion.2), channel_id=1, source_target_pairs={{0,240},{16,0},{32,16},{48,32},{64,48},{80,64},{96,80},{112,96},{1... | collective-permute-start | bytes 44072 | tf_op jit(solution)/shard_map/ppermute | solution.py:20
  100.2 1.2 collective-permute-done.7
  101.6 6.3 %collective-permute-start.8 = (f32[3,8,18]{2,1,0:T(8,128)S(1)}, f32[3,8,18]{2,1,0:T(8,128)S(1)}, u32[]{:S(2)}, u32[]{:S(2)}) collective-permute-start(f32[3,8,18]{2,1,0:T(8,128)S(1)} %pad_maximum_fusion.13), channel_id=1, source_target_pairs={{0,1},{1,0},{2,3},{3,2},{4,5},{5,4},{6,7},{7,6},{8,9},{9,8},{10,11... | collective-permute-start | bytes 5192 | tf_op jit(solution)/shard_map/ppermute | solution.py:20
  112.5 1.1 fusion.59
  113.9 2.3 collective-permute-start.9
  117.2 1.9 collective-permute-start.10
  119.2 4.1 %collective-permute-done.10 = f32[3,8,153]{2,1,0:T(8,128)S(1)} collective-permute-done((f32[3,8,153]{2,1,0:T(8,128)S(1)}, f32[3,8,153]{2,1,0:T(8,128)S(1)}, u32[]{:S(2)}, u32[]{:S(2)}) %collective-permute-start.10) | collective-permute-done | bytes 14720 | tf_op jit(solution)/shard_map/ppermute | solution.py:20
  123.5 2.1 collective-permute-start.11
  125.9 3.6 %collective-permute-done.11 = f32[3,8,34]{2,1,0:T(8,128)S(1)} collective-permute-done((f32[3,8,34]{2,1,0:T(8,128)S(1)}, f32[3,8,34]{2,1,0:T(8,128)S(1)}, u32[]{:S(2)}, u32[]{:S(2)}) %collective-permute-start.11) | collective-permute-done | bytes 3296 | tf_op jit(solution)/shard_map/ppermute | solution.py:20
  129.9 7.2 %scatter_fusion.1 = f32[3,8,128]{1,0,2:T(4,128)S(1)} fusion(f32[3,8,128]{1,0,2:T(4,128)S(1)} %copy.121, s32[178]{0:T(256)S(1)} %compare_select_fusion, f32[178,3,8]{2,1,0:T(4,128)S(1)} %copy.107), kind=kCustom, calls=%fused_computation.5 | custom fusion | flops 4272 | bytes 51976 | tf_op jit(solution)/shard_map/scatter-add | solution.py:149
  138.9 3.4 %collective-permute-start.12 = (f32[3,8,34]{2,1,0:T(8,128)S(1)}, f32[3,8,34]{2,1,0:T(8,128)S(1)}, u32[]{:S(2)}, u32[]{:S(2)}) collective-permute-start(f32[3,8,34]{2,1,0:T(8,128)S(1)} %pad_maximum_fusion.16), channel_id=1, source_target_pairs={{0,14},{2,0},{4,2},{6,4},{8,6},{10,8},{12,10},{14,12},{1,15},{3,1}... | collective-permute-start | bytes 9800 | tf_op jit(solution)/shard_map/ppermute | solution.py:20
  143.6 3.4 %collective-permute-start.13 = (f32[3,8,153]{2,1,0:T(8,128)S(1)}, f32[3,8,153]{2,1,0:T(8,128)S(1)}, u32[]{:S(2)}, u32[]{:S(2)}) collective-permute-start(f32[3,8,153]{2,1,0:T(8,128)S(1)} %pad_maximum_fusion.4), channel_id=1, source_target_pairs={{0,240},{16,0},{32,16},{48,32},{64,48},{80,64},{96,80},{112,96},{1... | collective-permute-start | bytes 44072 | tf_op jit(solution)/shard_map/ppermute | solution.py:20
  147.0 1.2 collective-permute-done.13
  148.3 6.3 %collective-permute-start.14 = (f32[3,8,18]{2,1,0:T(8,128)S(1)}, f32[3,8,18]{2,1,0:T(8,128)S(1)}, u32[]{:S(2)}, u32[]{:S(2)}) collective-permute-start(f32[3,8,18]{2,1,0:T(8,128)S(1)} %pad_maximum_fusion.17), channel_id=1, source_target_pairs={{0,1},{1,0},{2,3},{3,2},{4,5},{5,4},{6,7},{7,6},{8,9},{9,8},{10,11... | collective-permute-start | bytes 5192 | tf_op jit(solution)/shard_map/ppermute | solution.py:20
  159.2 1.1 fusion.61
  160.6 2.3 collective-permute-start.15
  164.0 1.9 collective-permute-start.16
  165.9 4.1 %collective-permute-done.16 = f32[3,8,153]{2,1,0:T(8,128)S(1)} collective-permute-done((f32[3,8,153]{2,1,0:T(8,128)S(1)}, f32[3,8,153]{2,1,0:T(8,128)S(1)}, u32[]{:S(2)}, u32[]{:S(2)}) %collective-permute-start.16) | collective-permute-done | bytes 14720 | tf_op jit(solution)/shard_map/ppermute | solution.py:20
  170.2 1.9 collective-permute-start.17
  172.4 3.7 %collective-permute-done.17 = f32[3,8,34]{2,1,0:T(8,128)S(1)} collective-permute-done((f32[3,8,34]{2,1,0:T(8,128)S(1)}, f32[3,8,34]{2,1,0:T(8,128)S(1)}, u32[]{:S(2)}, u32[]{:S(2)}) %collective-permute-start.17) | collective-permute-done | bytes 3296 | tf_op jit(solution)/shard_map/ppermute | solution.py:20
  176.6 7.2 %scatter_fusion.2 = f32[3,8,128]{1,0,2:T(4,128)S(1)} fusion(f32[3,8,128]{1,0,2:T(4,128)S(1)} %copy.122, s32[178]{0:T(256)S(1)} %compare_select_fusion, f32[178,3,8]{2,1,0:T(4,128)S(1)} %copy.112), kind=kCustom, calls=%fused_computation.6 | custom fusion | flops 4272 | bytes 51976 | tf_op jit(solution)/shard_map/scatter-add | solution.py:149
  186.2 3.4 %collective-permute-start.18 = (f32[3,8,34]{2,1,0:T(8,128)S(1)}, f32[3,8,34]{2,1,0:T(8,128)S(1)}, u32[]{:S(2)}, u32[]{:S(2)}) collective-permute-start(f32[3,8,34]{2,1,0:T(8,128)S(1)} %pad_maximum_fusion.20), channel_id=1, source_target_pairs={{0,14},{2,0},{4,2},{6,4},{8,6},{10,8},{12,10},{14,12},{1,15},{3,1}... | collective-permute-start | bytes 9800 | tf_op jit(solution)/shard_map/ppermute | solution.py:20
  190.9 3.4 %collective-permute-start.19 = (f32[3,8,153]{2,1,0:T(8,128)S(1)}, f32[3,8,153]{2,1,0:T(8,128)S(1)}, u32[]{:S(2)}, u32[]{:S(2)}) collective-permute-start(f32[3,8,153]{2,1,0:T(8,128)S(1)} %pad_maximum_fusion.6), channel_id=1, source_target_pairs={{0,240},{16,0},{32,16},{48,32},{64,48},{80,64},{96,80},{112,96},{1... | collective-permute-start | bytes 44072 | tf_op jit(solution)/shard_map/ppermute | solution.py:20
  194.3 1.2 collective-permute-done.19
  195.7 6.5 %collective-permute-start.20 = (f32[3,8,18]{2,1,0:T(8,128)S(1)}, f32[3,8,18]{2,1,0:T(8,128)S(1)}, u32[]{:S(2)}, u32[]{:S(2)}) collective-permute-start(f32[3,8,18]{2,1,0:T(8,128)S(1)} %pad_maximum_fusion.21), channel_id=1, source_target_pairs={{0,1},{1,0},{2,3},{3,2},{4,5},{5,4},{6,7},{7,6},{8,9},{9,8},{10,11... | collective-permute-start | bytes 5192 | tf_op jit(solution)/shard_map/ppermute | solution.py:20
  204.9 1.1 fusion.66
  207.5 1.1 fusion.57
  208.9 2.3 collective-permute-start.21
  212.2 1.9 collective-permute-start.22
  216.6 1.6 collective-permute-done.22
  218.4 1.9 collective-permute-start.23
  221.4 3.0 %collective-permute-done.23 = f32[3,8,34]{2,1,0:T(8,128)S(1)} collective-permute-done((f32[3,8,34]{2,1,0:T(8,128)S(1)}, f32[3,8,34]{2,1,0:T(8,128)S(1)}, u32[]{:S(2)}, u32[]{:S(2)}) %collective-permute-start.23) | collective-permute-done | bytes 3296 | tf_op jit(solution)/shard_map/ppermute | solution.py:20
  224.9 7.2 %scatter_fusion.3 = f32[3,8,128]{1,0,2:T(4,128)S(1)} fusion(f32[3,8,128]{1,0,2:T(4,128)S(1)} %copy.123, s32[178]{0:T(256)S(1)} %compare_select_fusion, f32[178,3,8]{2,1,0:T(4,128)S(1)} %copy.117), kind=kCustom, calls=%fused_computation.7 | custom fusion | flops 4272 | bytes 51976 | tf_op jit(solution)/shard_map/scatter-add | solution.py:149
  232.1 1.2 multiply_reduce_fusion
  234.1 21.7 %psum.21 = f32[3,2]{1,0:T(4,128)S(1)} all-reduce(f32[3,2]{1,0:T(4,128)S(1)} %pad_maximum_fusion.24), channel_id=1, replica_groups=mesh['runs'=2,'gx'=16,'gy'=8,'gz'=2] {'gx'}, use_global_device_ids=true, to_apply=%region_34.36 | all-reduce | flops 6 | bytes 48 | tf_op jit(solution)/shard_map/psum | solution.py:25
  255.8 11.9 %psum.22 = f32[3,2]{1,0:T(4,128)S(1)} all-reduce(f32[3,2]{1,0:T(4,128)S(1)} %psum.21), channel_id=1, replica_groups=mesh['runs'=2,'gx'=16,'gy'=8,'gz'=2] {'gy'}, use_global_device_ids=true, to_apply=%region_35.37 | all-reduce | flops 6 | bytes 48 | tf_op jit(solution)/shard_map/psum | solution.py:25
  267.8 15.8 %psum.23 = f32[3,2]{1,0:T(4,128)S(1)} all-reduce(f32[3,2]{1,0:T(4,128)S(1)} %psum.22), channel_id=1, replica_groups=mesh['runs'=2,'gx'=16,'gy'=8,'gz'=2] {'gz'}, use_global_device_ids=true, to_apply=%region_36.38 | all-reduce | flops 6 | bytes 48 | tf_op jit(solution)/shard_map/psum | solution.py:25
  (280 shorter events, 43.0 us)
Async XLA Ops:
  2.0 8.5 %copy-start.4 = (s32[2,1792]{1,0:T(2,128)S(1)}, s32[2,1792]{1,0:T(2,128)}, u32[]{:S(2)}) copy-start(s32[2,1792]{1,0:T(2,128)} %param.14) | copy-start | bytes 43012
  3.9 57.6 %copy-start.3 = (f32[3,178]{1,0:T(4,128)S(1)}, f32[3,178]{1,0:T(4,128)}, u32[]{:S(2)}) copy-start(f32[3,178]{1,0:T(4,128)} %constant.57.clone) | copy-start | bytes 6412
  3.9 57.7 %copy-start = (f32[3,8,128]{2,1,0:T(8,128)S(1)}, f32[3,8,128]{2,1,0:T(8,128)}, u32[]{:S(2)}) copy-start(f32[3,8,128]{2,1,0:T(8,128)} %param.11) | copy-start | bytes 36868
  4.1 7.1 %collective-permute-start = (f32[3,8,34]{2,1,0:T(8,128)S(1)}, f32[3,8,34]{2,1,0:T(8,128)S(1)}, u32[]{:S(2)}, u32[]{:S(2)}) collective-permute-start(f32[3,8,34]{2,1,0:T(8,128)S(1)} %pad_maximum_fusion.8), channel_id=1, source_target_pairs={{0,14},{2,0},{4,2},{6,4},{8,6},{10,8},{12,10},{14,12},{1,15},{3,1}... | collective-permute-start | bytes 9800 | tf_op jit(solution)/shard_map/ppermute | solution.py:20
  11.5 44.7 %collective-permute-start.1 = (f32[3,8,153]{2,1,0:T(8,128)S(1)}, f32[3,8,153]{2,1,0:T(8,128)S(1)}, u32[]{:S(2)}, u32[]{:S(2)}) collective-permute-start(f32[3,8,153]{2,1,0:T(8,128)S(1)} %pad_maximum_fusion), channel_id=1, source_target_pairs={{0,240},{16,0},{32,16},{48,32},{64,48},{80,64},{96,80},{112,96},{1... | collective-permute-start | bytes 44072 | tf_op jit(solution)/shard_map/ppermute | solution.py:20
  56.3 5.1 %collective-permute-start.2 = (f32[3,8,18]{2,1,0:T(8,128)S(1)}, f32[3,8,18]{2,1,0:T(8,128)S(1)}, u32[]{:S(2)}, u32[]{:S(2)}) collective-permute-start(f32[3,8,18]{2,1,0:T(8,128)S(1)} %pad_maximum_fusion.9), channel_id=1, source_target_pairs={{0,1},{1,0},{2,3},{3,2},{4,5},{5,4},{6,7},{7,6},{8,9},{9,8},{10,11... | collective-permute-start | bytes 5192 | tf_op jit(solution)/shard_map/ppermute | solution.py:20
  65.2 13.2 %copy-start.1 = (s32[7,128]{1,0:T(8,128)S(1)}, s32[7,128]{1,0:T(8,128)}, u32[]{:S(2)}) copy-start(s32[7,128]{1,0:T(8,128)} %param.15) | copy-start | bytes 10756
  66.6 3.1 %collective-permute-start.3 = (f32[3,8,18]{2,1,0:T(8,128)S(1)}, f32[3,8,18]{2,1,0:T(8,128)S(1)}, u32[]{:S(2)}, u32[]{:S(2)}) collective-permute-start(f32[3,8,18]{2,1,0:T(8,128)S(1)} %pad_maximum_fusion.10), channel_id=1, source_target_pairs={{0,1},{1,0},{2,3},{3,2},{4,5},{5,4},{6,7},{7,6},{8,9},{9,8},{10,11... | collective-permute-start | bytes 5192 | tf_op jit(solution)/shard_map/ppermute | solution.py:20
  69.9 6.4 %collective-permute-start.4 = (f32[3,8,153]{2,1,0:T(8,128)S(1)}, f32[3,8,153]{2,1,0:T(8,128)S(1)}, u32[]{:S(2)}, u32[]{:S(2)}) collective-permute-start(f32[3,8,153]{2,1,0:T(8,128)S(1)} %pad_maximum_fusion.1), channel_id=1, source_target_pairs={{0,16},{16,32},{32,48},{48,64},{64,80},{80,96},{96,112},{112,128},... | collective-permute-start | bytes 44072 | tf_op jit(solution)/shard_map/ppermute | solution.py:20
  76.5 6.2 %collective-permute-start.5 = (f32[3,8,34]{2,1,0:T(8,128)S(1)}, f32[3,8,34]{2,1,0:T(8,128)S(1)}, u32[]{:S(2)}, u32[]{:S(2)}) collective-permute-start(f32[3,8,34]{2,1,0:T(8,128)S(1)} %pad_maximum_fusion.11), channel_id=1, source_target_pairs={{0,2},{2,4},{4,6},{6,8},{8,10},{10,12},{12,14},{14,0},{1,3},{3,5},... | collective-permute-start | bytes 9800 | tf_op jit(solution)/shard_map/ppermute | solution.py:20
  78.7 11.7 %copy-start.5 = (f32[3,8,128]{2,1,0:T(8,128)S(1)}, f32[3,8,128]{2,1,0:T(8,128)}, u32[]{:S(2)}) copy-start(f32[3,8,128]{2,1,0:T(8,128)} %param.12) | copy-start | bytes 36868
  92.1 4.5 %collective-permute-start.6 = (f32[3,8,34]{2,1,0:T(8,128)S(1)}, f32[3,8,34]{2,1,0:T(8,128)S(1)}, u32[]{:S(2)}, u32[]{:S(2)}) collective-permute-start(f32[3,8,34]{2,1,0:T(8,128)S(1)} %pad_maximum_fusion.12), channel_id=1, source_target_pairs={{0,14},{2,0},{4,2},{6,4},{8,6},{10,8},{12,10},{14,12},{1,15},{3,1}... | collective-permute-start | bytes 9800 | tf_op jit(solution)/shard_map/ppermute | solution.py:20
  96.8 4.6 %collective-permute-start.7 = (f32[3,8,153]{2,1,0:T(8,128)S(1)}, f32[3,8,153]{2,1,0:T(8,128)S(1)}, u32[]{:S(2)}, u32[]{:S(2)}) collective-permute-start(f32[3,8,153]{2,1,0:T(8,128)S(1)} %pad_maximum_fusion.2), channel_id=1, source_target_pairs={{0,240},{16,0},{32,16},{48,32},{64,48},{80,64},{96,80},{112,96},{1... | collective-permute-start | bytes 44072 | tf_op jit(solution)/shard_map/ppermute | solution.py:20
  101.6 7.1 %collective-permute-start.8 = (f32[3,8,18]{2,1,0:T(8,128)S(1)}, f32[3,8,18]{2,1,0:T(8,128)S(1)}, u32[]{:S(2)}, u32[]{:S(2)}) collective-permute-start(f32[3,8,18]{2,1,0:T(8,128)S(1)} %pad_maximum_fusion.13), channel_id=1, source_target_pairs={{0,1},{1,0},{2,3},{3,2},{4,5},{5,4},{6,7},{7,6},{8,9},{9,8},{10,11... | collective-permute-start | bytes 5192 | tf_op jit(solution)/shard_map/ppermute | solution.py:20
  113.9 3.1 %collective-permute-start.9 = (f32[3,8,18]{2,1,0:T(8,128)S(1)}, f32[3,8,18]{2,1,0:T(8,128)S(1)}, u32[]{:S(2)}, u32[]{:S(2)}) collective-permute-start(f32[3,8,18]{2,1,0:T(8,128)S(1)} %pad_maximum_fusion.14), channel_id=1, source_target_pairs={{0,1},{1,0},{2,3},{3,2},{4,5},{5,4},{6,7},{7,6},{8,9},{9,8},{10,11... | collective-permute-start | bytes 5192 | tf_op jit(solution)/shard_map/ppermute | solution.py:20
  117.2 6.1 %collective-permute-start.10 = (f32[3,8,153]{2,1,0:T(8,128)S(1)}, f32[3,8,153]{2,1,0:T(8,128)S(1)}, u32[]{:S(2)}, u32[]{:S(2)}) collective-permute-start(f32[3,8,153]{2,1,0:T(8,128)S(1)} %pad_maximum_fusion.3), channel_id=1, source_target_pairs={{0,16},{16,32},{32,48},{48,64},{64,80},{80,96},{96,112},{112,128},... | collective-permute-start | bytes 44072 | tf_op jit(solution)/shard_map/ppermute | solution.py:20
  123.5 6.0 %collective-permute-start.11 = (f32[3,8,34]{2,1,0:T(8,128)S(1)}, f32[3,8,34]{2,1,0:T(8,128)S(1)}, u32[]{:S(2)}, u32[]{:S(2)}) collective-permute-start(f32[3,8,34]{2,1,0:T(8,128)S(1)} %pad_maximum_fusion.15), channel_id=1, source_target_pairs={{0,2},{2,4},{4,6},{6,8},{8,10},{10,12},{12,14},{14,0},{1,3},{3,5},... | collective-permute-start | bytes 9800 | tf_op jit(solution)/shard_map/ppermute | solution.py:20
  138.9 4.5 %collective-permute-start.12 = (f32[3,8,34]{2,1,0:T(8,128)S(1)}, f32[3,8,34]{2,1,0:T(8,128)S(1)}, u32[]{:S(2)}, u32[]{:S(2)}) collective-permute-start(f32[3,8,34]{2,1,0:T(8,128)S(1)} %pad_maximum_fusion.16), channel_id=1, source_target_pairs={{0,14},{2,0},{4,2},{6,4},{8,6},{10,8},{12,10},{14,12},{1,15},{3,1}... | collective-permute-start | bytes 9800 | tf_op jit(solution)/shard_map/ppermute | solution.py:20
  143.6 4.6 %collective-permute-start.13 = (f32[3,8,153]{2,1,0:T(8,128)S(1)}, f32[3,8,153]{2,1,0:T(8,128)S(1)}, u32[]{:S(2)}, u32[]{:S(2)}) collective-permute-start(f32[3,8,153]{2,1,0:T(8,128)S(1)} %pad_maximum_fusion.4), channel_id=1, source_target_pairs={{0,240},{16,0},{32,16},{48,32},{64,48},{80,64},{96,80},{112,96},{1... | collective-permute-start | bytes 44072 | tf_op jit(solution)/shard_map/ppermute | solution.py:20
  148.3 7.1 %collective-permute-start.14 = (f32[3,8,18]{2,1,0:T(8,128)S(1)}, f32[3,8,18]{2,1,0:T(8,128)S(1)}, u32[]{:S(2)}, u32[]{:S(2)}) collective-permute-start(f32[3,8,18]{2,1,0:T(8,128)S(1)} %pad_maximum_fusion.17), channel_id=1, source_target_pairs={{0,1},{1,0},{2,3},{3,2},{4,5},{5,4},{6,7},{7,6},{8,9},{9,8},{10,11... | collective-permute-start | bytes 5192 | tf_op jit(solution)/shard_map/ppermute | solution.py:20
  160.6 3.1 %collective-permute-start.15 = (f32[3,8,18]{2,1,0:T(8,128)S(1)}, f32[3,8,18]{2,1,0:T(8,128)S(1)}, u32[]{:S(2)}, u32[]{:S(2)}) collective-permute-start(f32[3,8,18]{2,1,0:T(8,128)S(1)} %pad_maximum_fusion.18), channel_id=1, source_target_pairs={{0,1},{1,0},{2,3},{3,2},{4,5},{5,4},{6,7},{7,6},{8,9},{9,8},{10,11... | collective-permute-start | bytes 5192 | tf_op jit(solution)/shard_map/ppermute | solution.py:20
  164.0 6.1 %collective-permute-start.16 = (f32[3,8,153]{2,1,0:T(8,128)S(1)}, f32[3,8,153]{2,1,0:T(8,128)S(1)}, u32[]{:S(2)}, u32[]{:S(2)}) collective-permute-start(f32[3,8,153]{2,1,0:T(8,128)S(1)} %pad_maximum_fusion.5), channel_id=1, source_target_pairs={{0,16},{16,32},{32,48},{48,64},{64,80},{80,96},{96,112},{112,128},... | collective-permute-start | bytes 44072 | tf_op jit(solution)/shard_map/ppermute | solution.py:20
  170.2 6.0 %collective-permute-start.17 = (f32[3,8,34]{2,1,0:T(8,128)S(1)}, f32[3,8,34]{2,1,0:T(8,128)S(1)}, u32[]{:S(2)}, u32[]{:S(2)}) collective-permute-start(f32[3,8,34]{2,1,0:T(8,128)S(1)} %pad_maximum_fusion.19), channel_id=1, source_target_pairs={{0,2},{2,4},{4,6},{6,8},{8,10},{10,12},{12,14},{14,0},{1,3},{3,5},... | collective-permute-start | bytes 9800 | tf_op jit(solution)/shard_map/ppermute | solution.py:20
  184.8 47.3 %copy-start.2 = (f32[3,8,128]{2,1,0:T(8,128)}, f32[3,8,128]{2,1,0:T(8,128)S(1)}, u32[]{:S(2)}) copy-start(f32[3,8,128]{2,1,0:T(8,128)S(1)} %pad_add_fusion) | copy-start | bytes 36868
  186.2 4.5 %collective-permute-start.18 = (f32[3,8,34]{2,1,0:T(8,128)S(1)}, f32[3,8,34]{2,1,0:T(8,128)S(1)}, u32[]{:S(2)}, u32[]{:S(2)}) collective-permute-start(f32[3,8,34]{2,1,0:T(8,128)S(1)} %pad_maximum_fusion.20), channel_id=1, source_target_pairs={{0,14},{2,0},{4,2},{6,4},{8,6},{10,8},{12,10},{14,12},{1,15},{3,1}... | collective-permute-start | bytes 9800 | tf_op jit(solution)/shard_map/ppermute | solution.py:20
  190.9 4.6 %collective-permute-start.19 = (f32[3,8,153]{2,1,0:T(8,128)S(1)}, f32[3,8,153]{2,1,0:T(8,128)S(1)}, u32[]{:S(2)}, u32[]{:S(2)}) collective-permute-start(f32[3,8,153]{2,1,0:T(8,128)S(1)} %pad_maximum_fusion.6), channel_id=1, source_target_pairs={{0,240},{16,0},{32,16},{48,32},{64,48},{80,64},{96,80},{112,96},{1... | collective-permute-start | bytes 44072 | tf_op jit(solution)/shard_map/ppermute | solution.py:20
  195.7 7.1 %collective-permute-start.20 = (f32[3,8,18]{2,1,0:T(8,128)S(1)}, f32[3,8,18]{2,1,0:T(8,128)S(1)}, u32[]{:S(2)}, u32[]{:S(2)}) collective-permute-start(f32[3,8,18]{2,1,0:T(8,128)S(1)} %pad_maximum_fusion.21), channel_id=1, source_target_pairs={{0,1},{1,0},{2,3},{3,2},{4,5},{5,4},{6,7},{7,6},{8,9},{9,8},{10,11... | collective-permute-start | bytes 5192 | tf_op jit(solution)/shard_map/ppermute | solution.py:20
  208.9 3.1 %collective-permute-start.21 = (f32[3,8,18]{2,1,0:T(8,128)S(1)}, f32[3,8,18]{2,1,0:T(8,128)S(1)}, u32[]{:S(2)}, u32[]{:S(2)}) collective-permute-start(f32[3,8,18]{2,1,0:T(8,128)S(1)} %pad_maximum_fusion.22), channel_id=1, source_target_pairs={{0,1},{1,0},{2,3},{3,2},{4,5},{5,4},{6,7},{7,6},{8,9},{9,8},{10,11... | collective-permute-start | bytes 5192 | tf_op jit(solution)/shard_map/ppermute | solution.py:20
  212.2 6.1 %collective-permute-start.22 = (f32[3,8,153]{2,1,0:T(8,128)S(1)}, f32[3,8,153]{2,1,0:T(8,128)S(1)}, u32[]{:S(2)}, u32[]{:S(2)}) collective-permute-start(f32[3,8,153]{2,1,0:T(8,128)S(1)} %pad_maximum_fusion.7), channel_id=1, source_target_pairs={{0,16},{16,32},{32,48},{48,64},{64,80},{80,96},{96,112},{112,128},... | collective-permute-start | bytes 44072 | tf_op jit(solution)/shard_map/ppermute | solution.py:20
  218.4 6.0 %collective-permute-start.23 = (f32[3,8,34]{2,1,0:T(8,128)S(1)}, f32[3,8,34]{2,1,0:T(8,128)S(1)}, u32[]{:S(2)}, u32[]{:S(2)}) collective-permute-start(f32[3,8,34]{2,1,0:T(8,128)S(1)} %pad_maximum_fusion.23), channel_id=1, source_target_pairs={{0,2},{2,4},{4,6},{6,8},{8,10},{10,12},{12,14},{14,0},{1,3},{3,5},... | collective-permute-start | bytes 9800 | tf_op jit(solution)/shard_map/ppermute | solution.py:20
where the time goes:
time: 285 us; the launch traced here: 284 us
  starting transfers between devices  119 us (42%)
  blocking collectives  49.5 us (17%)
  waiting for transfers between devices  42.6 us (15%)
  other arithmetic  38.8 us (14%)
  matrix products  15.5 us (5%)
  local copies, waits for them, and re-layouts  13.6 us (5%)
  between operations  5.59 us (2%)
    ppermute x24, starting transfers between devices, from_behind(): lax.ppermute(value, axis, [(i, (i + by) % count) for i in range(count)])  119 us
    psum x3, blocking collectives, over_axes(): value = lax.psum(value, axis)  49.5 us
    ppermute x24, waiting for transfers between devices, from_behind(): lax.ppermute(value, axis, [(i, (i + by) % count) for i in range(count)])  42.6 us
    scatter-add x4, other arithmetic, local_forces(): home_forces = forces[:, :, :cluster_count].at[:, :, send_list].add(returned)  28.6 us
  transfers between devices with their start and end apart: 24, of which 24 were waited for; matrix products, arithmetic and copies ran while one was open for 1% of the time, Pallas kernels for 0%

commit v1 on v0

--- a/solution.py
+++ b/solution.py
@@ -22,7 +22,7 @@
 
 def over_axes(value, axes):
     for axis in axes:
-        value = lax.psum(value, axis)
+        value = jnp.sum(lax.all_gather(value, axis), 0)
     return value
 
 

time: 285 us -> 283 us (level)
    psum x3 -> x0, blocking collectives: 49.5 us -> none  [over_axes(): value = lax.psum(value, axis)]
    all_gather x0 -> x3, blocking collectives: none -> 46.9 us  [over_axes(): value = jnp.sum(lax.all_gather(value, axis), 0)]
where the time goes in v1:
time: 283 us; the launch traced here: 282 us
  starting transfers between devices  119 us (42%)
  blocking collectives  46.9 us (17%)
  waiting for transfers between devices  42.6 us (15%)
  other arithmetic  39.4 us (14%)
  matrix products  15.5 us (5%)
  local copies, waits for them, and re-layouts  13 us (5%)
  between operations  5.59 us (2%)
    ppermute x24, starting transfers between devices, from_behind(): lax.ppermute(value, axis, [(i, (i + by) % count) for i in range(count)])  119 us
    all_gather x3, blocking collectives, over_axes(): value = jnp.sum(lax.all_gather(value, axis), 0)  46.9 us
    ppermute x24, waiting for transfers between devices, from_behind(): lax.ppermute(value, axis, [(i, (i + by) % count) for i in range(count)])  42.6 us
    scatter-add x4, other arithmetic, local_forces(): home_forces = forces[:, :, :cluster_count].at[:, :, send_list].add(returned)  28.6 us
  transfers between devices with their start and end apart: 24, of which 24 were waited for; matrix products, arithmetic and copies ran while one was open for 1% of the time, Pallas kernels for 0%

profile of v1, /device:TPU:65, one launch (start us, length us, event | category | flops | bytes accessed | tf_op | source)
XLA Modules:
  0.0 281.8 jit_solution(11140984390668547287)
XLA Ops:
  4.1 6.3 %collective-permute-start = (f32[3,8,34]{2,1,0:T(8,128)S(1)}, f32[3,8,34]{2,1,0:T(8,128)S(1)}, u32[]{:S(2)}, u32[]{:S(2)}) collective-permute-start(f32[3,8,34]{2,1,0:T(8,128)S(1)} %pad_maximum_fusion.8), channel_id=1, source_target_pairs={{0,14},{2,0},{4,2},{6,4},{8,6},{10,8},{12,10},{14,12},{1,15},{3,1}... | collective-permute-start | bytes 9800 | tf_op jit(solution)/shard_map/ppermute | solution.py:20
  11.5 43.7 %collective-permute-start.1 = (f32[3,8,153]{2,1,0:T(8,128)S(1)}, f32[3,8,153]{2,1,0:T(8,128)S(1)}, u32[]{:S(2)}, u32[]{:S(2)}) collective-permute-start(f32[3,8,153]{2,1,0:T(8,128)S(1)} %pad_maximum_fusion), channel_id=1, source_target_pairs={{0,240},{16,0},{32,16},{48,32},{64,48},{80,64},{96,80},{112,96},{1... | collective-permute-start | bytes 44072 | tf_op jit(solution)/shard_map/ppermute | solution.py:20
  56.3 4.2 %collective-permute-start.2 = (f32[3,8,18]{2,1,0:T(8,128)S(1)}, f32[3,8,18]{2,1,0:T(8,128)S(1)}, u32[]{:S(2)}, u32[]{:S(2)}) collective-permute-start(f32[3,8,18]{2,1,0:T(8,128)S(1)} %pad_maximum_fusion.9), channel_id=1, source_target_pairs={{0,1},{1,0},{2,3},{3,2},{4,5},{5,4},{6,7},{7,6},{8,9},{9,8},{10,11... | collective-permute-start | bytes 5192 | tf_op jit(solution)/shard_map/ppermute | solution.py:20
  65.2 1.1 fusion.55
  66.6 2.3 collective-permute-start.3
  69.9 1.9 collective-permute-start.4
  71.9 4.4 %collective-permute-done.4 = f32[3,8,153]{2,1,0:T(8,128)S(1)} collective-permute-done((f32[3,8,153]{2,1,0:T(8,128)S(1)}, f32[3,8,153]{2,1,0:T(8,128)S(1)}, u32[]{:S(2)}, u32[]{:S(2)}) %collective-permute-start.4) | collective-permute-done | bytes 14720 | tf_op jit(solution)/shard_map/ppermute | solution.py:20
  76.5 1.9 collective-permute-start.5
  78.7 4.0 %collective-permute-done.5 = f32[3,8,34]{2,1,0:T(8,128)S(1)} collective-permute-done((f32[3,8,34]{2,1,0:T(8,128)S(1)}, f32[3,8,34]{2,1,0:T(8,128)S(1)}, u32[]{:S(2)}, u32[]{:S(2)}) %collective-permute-start.5) | collective-permute-done | bytes 3296 | tf_op jit(solution)/shard_map/ppermute | solution.py:20
  83.2 7.2 %scatter_fusion = f32[3,8,128]{1,0,2:T(4,128)S(1)} fusion(f32[3,8,128]{1,0,2:T(4,128)S(1)} %copy.120, s32[178]{0:T(256)S(1)} %compare_select_fusion, f32[178,3,8]{2,1,0:T(4,128)S(1)} %copy.102), kind=kCustom, calls=%fused_computation.4 | custom fusion | flops 4272 | bytes 51976 | tf_op jit(solution)/shard_map/scatter-add | solution.py:149
  92.1 3.4 %collective-permute-start.6 = (f32[3,8,34]{2,1,0:T(8,128)S(1)}, f32[3,8,34]{2,1,0:T(8,128)S(1)}, u32[]{:S(2)}, u32[]{:S(2)}) collective-permute-start(f32[3,8,34]{2,1,0:T(8,128)S(1)} %pad_maximum_fusion.12), channel_id=1, source_target_pairs={{0,14},{2,0},{4,2},{6,4},{8,6},{10,8},{12,10},{14,12},{1,15},{3,1}... | collective-permute-start | bytes 9800 | tf_op jit(solution)/shard_map/ppermute | solution.py:20
  96.8 3.4 %collective-permute-start.7 = (f32[3,8,153]{2,1,0:T(8,128)S(1)}, f32[3,8,153]{2,1,0:T(8,128)S(1)}, u32[]{:S(2)}, u32[]{:S(2)}) collective-permute-start(f32[3,8,153]{2,1,0:T(8,128)S(1)} %pad_maximum_fusion.2), channel_id=1, source_target_pairs={{0,240},{16,0},{32,16},{48,32},{64,48},{80,64},{96,80},{112,96},{1... | collective-permute-start | bytes 44072 | tf_op jit(solution)/shard_map/ppermute | solution.py:20
  100.2 1.2 collective-permute-done.7
  101.6 6.3 %collective-permute-start.8 = (f32[3,8,18]{2,1,0:T(8,128)S(1)}, f32[3,8,18]{2,1,0:T(8,128)S(1)}, u32[]{:S(2)}, u32[]{:S(2)}) collective-permute-start(f32[3,8,18]{2,1,0:T(8,128)S(1)} %pad_maximum_fusion.13), channel_id=1, source_target_pairs={{0,1},{1,0},{2,3},{3,2},{4,5},{5,4},{6,7},{7,6},{8,9},{9,8},{10,11... | collective-permute-start | bytes 5192 | tf_op jit(solution)/shard_map/ppermute | solution.py:20
  112.5 1.1 fusion.59
  113.9 2.3 collective-permute-start.9
  117.2 1.9 collective-permute-start.10
  119.2 4.1 %collective-permute-done.10 = f32[3,8,153]{2,1,0:T(8,128)S(1)} collective-permute-done((f32[3,8,153]{2,1,0:T(8,128)S(1)}, f32[3,8,153]{2,1,0:T(8,128)S(1)}, u32[]{:S(2)}, u32[]{:S(2)}) %collective-permute-start.10) | collective-permute-done | bytes 14720 | tf_op jit(solution)/shard_map/ppermute | solution.py:20
  123.5 2.1 collective-permute-start.11
  125.9 3.6 %collective-permute-done.11 = f32[3,8,34]{2,1,0:T(8,128)S(1)} collective-permute-done((f32[3,8,34]{2,1,0:T(8,128)S(1)}, f32[3,8,34]{2,1,0:T(8,128)S(1)}, u32[]{:S(2)}, u32[]{:S(2)}) %collective-permute-start.11) | collective-permute-done | bytes 3296 | tf_op jit(solution)/shard_map/ppermute | solution.py:20
  129.9 7.2 %scatter_fusion.1 = f32[3,8,128]{1,0,2:T(4,128)S(1)} fusion(f32[3,8,128]{1,0,2:T(4,128)S(1)} %copy.121, s32[178]{0:T(256)S(1)} %compare_select_fusion, f32[178,3,8]{2,1,0:T(4,128)S(1)} %copy.107), kind=kCustom, calls=%fused_computation.5 | custom fusion | flops 4272 | bytes 51976 | tf_op jit(solution)/shard_map/scatter-add | solution.py:149
  138.9 3.4 %collective-permute-start.12 = (f32[3,8,34]{2,1,0:T(8,128)S(1)}, f32[3,8,34]{2,1,0:T(8,128)S(1)}, u32[]{:S(2)}, u32[]{:S(2)}) collective-permute-start(f32[3,8,34]{2,1,0:T(8,128)S(1)} %pad_maximum_fusion.16), channel_id=1, source_target_pairs={{0,14},{2,0},{4,2},{6,4},{8,6},{10,8},{12,10},{14,12},{1,15},{3,1}... | collective-permute-start | bytes 9800 | tf_op jit(solution)/shard_map/ppermute | solution.py:20
  143.6 3.4 %collective-permute-start.13 = (f32[3,8,153]{2,1,0:T(8,128)S(1)}, f32[3,8,153]{2,1,0:T(8,128)S(1)}, u32[]{:S(2)}, u32[]{:S(2)}) collective-permute-start(f32[3,8,153]{2,1,0:T(8,128)S(1)} %pad_maximum_fusion.4), channel_id=1, source_target_pairs={{0,240},{16,0},{32,16},{48,32},{64,48},{80,64},{96,80},{112,96},{1... | collective-permute-start | bytes 44072 | tf_op jit(solution)/shard_map/ppermute | solution.py:20
  147.0 1.2 collective-permute-done.13
  148.3 6.3 %collective-permute-start.14 = (f32[3,8,18]{2,1,0:T(8,128)S(1)}, f32[3,8,18]{2,1,0:T(8,128)S(1)}, u32[]{:S(2)}, u32[]{:S(2)}) collective-permute-start(f32[3,8,18]{2,1,0:T(8,128)S(1)} %pad_maximum_fusion.17), channel_id=1, source_target_pairs={{0,1},{1,0},{2,3},{3,2},{4,5},{5,4},{6,7},{7,6},{8,9},{9,8},{10,11... | collective-permute-start | bytes 5192 | tf_op jit(solution)/shard_map/ppermute | solution.py:20
  159.3 1.1 fusion.61
  160.6 2.3 collective-permute-start.15
  164.0 1.9 collective-permute-start.16
  165.9 4.1 %collective-permute-done.16 = f32[3,8,153]{2,1,0:T(8,128)S(1)} collective-permute-done((f32[3,8,153]{2,1,0:T(8,128)S(1)}, f32[3,8,153]{2,1,0:T(8,128)S(1)}, u32[]{:S(2)}, u32[]{:S(2)}) %collective-permute-start.16) | collective-permute-done | bytes 14720 | tf_op jit(solution)/shard_map/ppermute | solution.py:20
  170.2 1.9 collective-permute-start.17
  172.4 3.7 %collective-permute-done.17 = f32[3,8,34]{2,1,0:T(8,128)S(1)} collective-permute-done((f32[3,8,34]{2,1,0:T(8,128)S(1)}, f32[3,8,34]{2,1,0:T(8,128)S(1)}, u32[]{:S(2)}, u32[]{:S(2)}) %collective-permute-start.17) | collective-permute-done | bytes 3296 | tf_op jit(solution)/shard_map/ppermute | solution.py:20
  176.6 7.2 %scatter_fusion.2 = f32[3,8,128]{1,0,2:T(4,128)S(1)} fusion(f32[3,8,128]{1,0,2:T(4,128)S(1)} %copy.122, s32[178]{0:T(256)S(1)} %compare_select_fusion, f32[178,3,8]{2,1,0:T(4,128)S(1)} %copy.112), kind=kCustom, calls=%fused_computation.6 | custom fusion | flops 4272 | bytes 51976 | tf_op jit(solution)/shard_map/scatter-add | solution.py:149
  186.2 3.4 %collective-permute-start.18 = (f32[3,8,34]{2,1,0:T(8,128)S(1)}, f32[3,8,34]{2,1,0:T(8,128)S(1)}, u32[]{:S(2)}, u32[]{:S(2)}) collective-permute-start(f32[3,8,34]{2,1,0:T(8,128)S(1)} %pad_maximum_fusion.20), channel_id=1, source_target_pairs={{0,14},{2,0},{4,2},{6,4},{8,6},{10,8},{12,10},{14,12},{1,15},{3,1}... | collective-permute-start | bytes 9800 | tf_op jit(solution)/shard_map/ppermute | solution.py:20
  190.9 3.4 %collective-permute-start.19 = (f32[3,8,153]{2,1,0:T(8,128)S(1)}, f32[3,8,153]{2,1,0:T(8,128)S(1)}, u32[]{:S(2)}, u32[]{:S(2)}) collective-permute-start(f32[3,8,153]{2,1,0:T(8,128)S(1)} %pad_maximum_fusion.6), channel_id=1, source_target_pairs={{0,240},{16,0},{32,16},{48,32},{64,48},{80,64},{96,80},{112,96},{1... | collective-permute-start | bytes 44072 | tf_op jit(solution)/shard_map/ppermute | solution.py:20
  194.3 1.2 collective-permute-done.19
  195.7 6.5 %collective-permute-start.20 = (f32[3,8,18]{2,1,0:T(8,128)S(1)}, f32[3,8,18]{2,1,0:T(8,128)S(1)}, u32[]{:S(2)}, u32[]{:S(2)}) collective-permute-start(f32[3,8,18]{2,1,0:T(8,128)S(1)} %pad_maximum_fusion.21), channel_id=1, source_target_pairs={{0,1},{1,0},{2,3},{3,2},{4,5},{5,4},{6,7},{7,6},{8,9},{9,8},{10,11... | collective-permute-start | bytes 5192 | tf_op jit(solution)/shard_map/ppermute | solution.py:20
  204.9 1.1 fusion.66
  207.5 1.1 fusion.57
  208.9 2.3 collective-permute-start.21
  212.2 1.9 collective-permute-start.22
  216.6 1.6 collective-permute-done.22
  218.4 1.9 collective-permute-start.23
  221.4 3.0 %collective-permute-done.23 = f32[3,8,34]{2,1,0:T(8,128)S(1)} collective-permute-done((f32[3,8,34]{2,1,0:T(8,128)S(1)}, f32[3,8,34]{2,1,0:T(8,128)S(1)}, u32[]{:S(2)}, u32[]{:S(2)}) %collective-permute-start.23) | collective-permute-done | bytes 3296 | tf_op jit(solution)/shard_map/ppermute | solution.py:20
  224.9 7.2 %scatter_fusion.3 = f32[3,8,128]{1,0,2:T(4,128)S(1)} fusion(f32[3,8,128]{1,0,2:T(4,128)S(1)} %copy.123, s32[178]{0:T(256)S(1)} %compare_select_fusion, f32[178,3,8]{2,1,0:T(4,128)S(1)} %copy.117), kind=kCustom, calls=%fused_computation.7 | custom fusion | flops 4272 | bytes 51976 | tf_op jit(solution)/shard_map/scatter-add | solution.py:149
  232.1 1.2 multiply_reduce_fusion
  234.2 20.7 %all-gather.3 = f32[16,3,2]{1,2,0:T(2,128)S(1)} all-gather(f32[1,3,2]{1,2,0:T(2,128)S(1)} %bitcast.84), channel_id=2, replica_groups=mesh['runs'=2,'gx'=16,'gy'=8,'gz'=2] {'gx'}, dimensions={0}, use_global_device_ids=true | all-gather | bytes 408 | tf_op jit(solution)/shard_map/all_gather | solution.py:25
  255.0 11.0 %all-gather.4 = f32[8,3,2]{1,2,0:T(2,128)S(1)} all-gather(f32[1,3,2]{1,2,0:T(2,128)S(1)} %bitcast.85), channel_id=3, replica_groups=mesh['runs'=2,'gx'=16,'gy'=8,'gz'=2] {'gy'}, dimensions={0}, use_global_device_ids=true | all-gather | bytes 216 | tf_op jit(solution)/shard_map/all_gather | solution.py:25
  266.0 15.1 %all-gather.5 = f32[2,3,2]{1,2,0:T(2,128)S(1)} all-gather(f32[1,3,2]{1,2,0:T(2,128)S(1)} %bitcast.86), channel_id=4, replica_groups=mesh['runs'=2,'gx'=16,'gy'=8,'gz'=2] {'gz'}, dimensions={0}, use_global_device_ids=true | all-gather | bytes 72 | tf_op jit(solution)/shard_map/all_gather | solution.py:25
  (283 shorter events, 43.1 us)
Async XLA Ops:
  2.0 8.5 %copy-start.4 = (s32[2,1792]{1,0:T(2,128)S(1)}, s32[2,1792]{1,0:T(2,128)}, u32[]{:S(2)}) copy-start(s32[2,1792]{1,0:T(2,128)} %param.14) | copy-start | bytes 43012
  3.9 57.6 %copy-start.3 = (f32[3,178]{1,0:T(4,128)S(1)}, f32[3,178]{1,0:T(4,128)}, u32[]{:S(2)}) copy-start(f32[3,178]{1,0:T(4,128)} %constant.57.clone) | copy-start | bytes 6412
  3.9 57.7 %copy-start = (f32[3,8,128]{2,1,0:T(8,128)S(1)}, f32[3,8,128]{2,1,0:T(8,128)}, u32[]{:S(2)}) copy-start(f32[3,8,128]{2,1,0:T(8,128)} %param.11) | copy-start | bytes 36868
  4.1 7.1 %collective-permute-start = (f32[3,8,34]{2,1,0:T(8,128)S(1)}, f32[3,8,34]{2,1,0:T(8,128)S(1)}, u32[]{:S(2)}, u32[]{:S(2)}) collective-permute-start(f32[3,8,34]{2,1,0:T(8,128)S(1)} %pad_maximum_fusion.8), channel_id=1, source_target_pairs={{0,14},{2,0},{4,2},{6,4},{8,6},{10,8},{12,10},{14,12},{1,15},{3,1}... | collective-permute-start | bytes 9800 | tf_op jit(solution)/shard_map/ppermute | solution.py:20
  11.5 44.7 %collective-permute-start.1 = (f32[3,8,153]{2,1,0:T(8,128)S(1)}, f32[3,8,153]{2,1,0:T(8,128)S(1)}, u32[]{:S(2)}, u32[]{:S(2)}) collective-permute-start(f32[3,8,153]{2,1,0:T(8,128)S(1)} %pad_maximum_fusion), channel_id=1, source_target_pairs={{0,240},{16,0},{32,16},{48,32},{64,48},{80,64},{96,80},{112,96},{1... | collective-permute-start | bytes 44072 | tf_op jit(solution)/shard_map/ppermute | solution.py:20
  56.3 5.1 %collective-permute-start.2 = (f32[3,8,18]{2,1,0:T(8,128)S(1)}, f32[3,8,18]{2,1,0:T(8,128)S(1)}, u32[]{:S(2)}, u32[]{:S(2)}) collective-permute-start(f32[3,8,18]{2,1,0:T(8,128)S(1)} %pad_maximum_fusion.9), channel_id=1, source_target_pairs={{0,1},{1,0},{2,3},{3,2},{4,5},{5,4},{6,7},{7,6},{8,9},{9,8},{10,11... | collective-permute-start | bytes 5192 | tf_op jit(solution)/shard_map/ppermute | solution.py:20
  65.2 13.2 %copy-start.1 = (s32[7,128]{1,0:T(8,128)S(1)}, s32[7,128]{1,0:T(8,128)}, u32[]{:S(2)}) copy-start(s32[7,128]{1,0:T(8,128)} %param.15) | copy-start | bytes 10756
  66.6 3.1 %collective-permute-start.3 = (f32[3,8,18]{2,1,0:T(8,128)S(1)}, f32[3,8,18]{2,1,0:T(8,128)S(1)}, u32[]{:S(2)}, u32[]{:S(2)}) collective-permute-start(f32[3,8,18]{2,1,0:T(8,128)S(1)} %pad_maximum_fusion.10), channel_id=1, source_target_pairs={{0,1},{1,0},{2,3},{3,2},{4,5},{5,4},{6,7},{7,6},{8,9},{9,8},{10,11... | collective-permute-start | bytes 5192 | tf_op jit(solution)/shard_map/ppermute | solution.py:20
  69.9 6.4 %collective-permute-start.4 = (f32[3,8,153]{2,1,0:T(8,128)S(1)}, f32[3,8,153]{2,1,0:T(8,128)S(1)}, u32[]{:S(2)}, u32[]{:S(2)}) collective-permute-start(f32[3,8,153]{2,1,0:T(8,128)S(1)} %pad_maximum_fusion.1), channel_id=1, source_target_pairs={{0,16},{16,32},{32,48},{48,64},{64,80},{80,96},{96,112},{112,128},... | collective-permute-start | bytes 44072 | tf_op jit(solution)/shard_map/ppermute | solution.py:20
  76.5 6.2 %collective-permute-start.5 = (f32[3,8,34]{2,1,0:T(8,128)S(1)}, f32[3,8,34]{2,1,0:T(8,128)S(1)}, u32[]{:S(2)}, u32[]{:S(2)}) collective-permute-start(f32[3,8,34]{2,1,0:T(8,128)S(1)} %pad_maximum_fusion.11), channel_id=1, source_target_pairs={{0,2},{2,4},{4,6},{6,8},{8,10},{10,12},{12,14},{14,0},{1,3},{3,5},... | collective-permute-start | bytes 9800 | tf_op jit(solution)/shard_map/ppermute | solution.py:20
  78.7 11.7 %copy-start.5 = (f32[3,8,128]{2,1,0:T(8,128)S(1)}, f32[3,8,128]{2,1,0:T(8,128)}, u32[]{:S(2)}) copy-start(f32[3,8,128]{2,1,0:T(8,128)} %param.12) | copy-start | bytes 36868
  92.1 4.5 %collective-permute-start.6 = (f32[3,8,34]{2,1,0:T(8,128)S(1)}, f32[3,8,34]{2,1,0:T(8,128)S(1)}, u32[]{:S(2)}, u32[]{:S(2)}) collective-permute-start(f32[3,8,34]{2,1,0:T(8,128)S(1)} %pad_maximum_fusion.12), channel_id=1, source_target_pairs={{0,14},{2,0},{4,2},{6,4},{8,6},{10,8},{12,10},{14,12},{1,15},{3,1}... | collective-permute-start | bytes 9800 | tf_op jit(solution)/shard_map/ppermute | solution.py:20
  96.8 4.6 %collective-permute-start.7 = (f32[3,8,153]{2,1,0:T(8,128)S(1)}, f32[3,8,153]{2,1,0:T(8,128)S(1)}, u32[]{:S(2)}, u32[]{:S(2)}) collective-permute-start(f32[3,8,153]{2,1,0:T(8,128)S(1)} %pad_maximum_fusion.2), channel_id=1, source_target_pairs={{0,240},{16,0},{32,16},{48,32},{64,48},{80,64},{96,80},{112,96},{1... | collective-permute-start | bytes 44072 | tf_op jit(solution)/shard_map/ppermute | solution.py:20
  101.6 7.1 %collective-permute-start.8 = (f32[3,8,18]{2,1,0:T(8,128)S(1)}, f32[3,8,18]{2,1,0:T(8,128)S(1)}, u32[]{:S(2)}, u32[]{:S(2)}) collective-permute-start(f32[3,8,18]{2,1,0:T(8,128)S(1)} %pad_maximum_fusion.13), channel_id=1, source_target_pairs={{0,1},{1,0},{2,3},{3,2},{4,5},{5,4},{6,7},{7,6},{8,9},{9,8},{10,11... | collective-permute-start | bytes 5192 | tf_op jit(solution)/shard_map/ppermute | solution.py:20
  113.9 3.1 %collective-permute-start.9 = (f32[3,8,18]{2,1,0:T(8,128)S(1)}, f32[3,8,18]{2,1,0:T(8,128)S(1)}, u32[]{:S(2)}, u32[]{:S(2)}) collective-permute-start(f32[3,8,18]{2,1,0:T(8,128)S(1)} %pad_maximum_fusion.14), channel_id=1, source_target_pairs={{0,1},{1,0},{2,3},{3,2},{4,5},{5,4},{6,7},{7,6},{8,9},{9,8},{10,11... | collective-permute-start | bytes 5192 | tf_op jit(solution)/shard_map/ppermute | solution.py:20
  117.2 6.1 %collective-permute-start.10 = (f32[3,8,153]{2,1,0:T(8,128)S(1)}, f32[3,8,153]{2,1,0:T(8,128)S(1)}, u32[]{:S(2)}, u32[]{:S(2)}) collective-permute-start(f32[3,8,153]{2,1,0:T(8,128)S(1)} %pad_maximum_fusion.3), channel_id=1, source_target_pairs={{0,16},{16,32},{32,48},{48,64},{64,80},{80,96},{96,112},{112,128},... | collective-permute-start | bytes 44072 | tf_op jit(solution)/shard_map/ppermute | solution.py:20
  123.5 6.0 %collective-permute-start.11 = (f32[3,8,34]{2,1,0:T(8,128)S(1)}, f32[3,8,34]{2,1,0:T(8,128)S(1)}, u32[]{:S(2)}, u32[]{:S(2)}) collective-permute-start(f32[3,8,34]{2,1,0:T(8,128)S(1)} %pad_maximum_fusion.15), channel_id=1, source_target_pairs={{0,2},{2,4},{4,6},{6,8},{8,10},{10,12},{12,14},{14,0},{1,3},{3,5},... | collective-permute-start | bytes 9800 | tf_op jit(solution)/shard_map/ppermute | solution.py:20
  138.9 4.5 %collective-permute-start.12 = (f32[3,8,34]{2,1,0:T(8,128)S(1)}, f32[3,8,34]{2,1,0:T(8,128)S(1)}, u32[]{:S(2)}, u32[]{:S(2)}) collective-permute-start(f32[3,8,34]{2,1,0:T(8,128)S(1)} %pad_maximum_fusion.16), channel_id=1, source_target_pairs={{0,14},{2,0},{4,2},{6,4},{8,6},{10,8},{12,10},{14,12},{1,15},{3,1}... | collective-permute-start | bytes 9800 | tf_op jit(solution)/shard_map/ppermute | solution.py:20
  143.6 4.6 %collective-permute-start.13 = (f32[3,8,153]{2,1,0:T(8,128)S(1)}, f32[3,8,153]{2,1,0:T(8,128)S(1)}, u32[]{:S(2)}, u32[]{:S(2)}) collective-permute-start(f32[3,8,153]{2,1,0:T(8,128)S(1)} %pad_maximum_fusion.4), channel_id=1, source_target_pairs={{0,240},{16,0},{32,16},{48,32},{64,48},{80,64},{96,80},{112,96},{1... | collective-permute-start | bytes 44072 | tf_op jit(solution)/shard_map/ppermute | solution.py:20
  148.3 7.1 %collective-permute-start.14 = (f32[3,8,18]{2,1,0:T(8,128)S(1)}, f32[3,8,18]{2,1,0:T(8,128)S(1)}, u32[]{:S(2)}, u32[]{:S(2)}) collective-permute-start(f32[3,8,18]{2,1,0:T(8,128)S(1)} %pad_maximum_fusion.17), channel_id=1, source_target_pairs={{0,1},{1,0},{2,3},{3,2},{4,5},{5,4},{6,7},{7,6},{8,9},{9,8},{10,11... | collective-permute-start | bytes 5192 | tf_op jit(solution)/shard_map/ppermute | solution.py:20
  160.6 3.1 %collective-permute-start.15 = (f32[3,8,18]{2,1,0:T(8,128)S(1)}, f32[3,8,18]{2,1,0:T(8,128)S(1)}, u32[]{:S(2)}, u32[]{:S(2)}) collective-permute-start(f32[3,8,18]{2,1,0:T(8,128)S(1)} %pad_maximum_fusion.18), channel_id=1, source_target_pairs={{0,1},{1,0},{2,3},{3,2},{4,5},{5,4},{6,7},{7,6},{8,9},{9,8},{10,11... | collective-permute-start | bytes 5192 | tf_op jit(solution)/shard_map/ppermute | solution.py:20
  164.0 6.1 %collective-permute-start.16 = (f32[3,8,153]{2,1,0:T(8,128)S(1)}, f32[3,8,153]{2,1,0:T(8,128)S(1)}, u32[]{:S(2)}, u32[]{:S(2)}) collective-permute-start(f32[3,8,153]{2,1,0:T(8,128)S(1)} %pad_maximum_fusion.5), channel_id=1, source_target_pairs={{0,16},{16,32},{32,48},{48,64},{64,80},{80,96},{96,112},{112,128},... | collective-permute-start | bytes 44072 | tf_op jit(solution)/shard_map/ppermute | solution.py:20
  170.2 6.0 %collective-permute-start.17 = (f32[3,8,34]{2,1,0:T(8,128)S(1)}, f32[3,8,34]{2,1,0:T(8,128)S(1)}, u32[]{:S(2)}, u32[]{:S(2)}) collective-permute-start(f32[3,8,34]{2,1,0:T(8,128)S(1)} %pad_maximum_fusion.19), channel_id=1, source_target_pairs={{0,2},{2,4},{4,6},{6,8},{8,10},{10,12},{12,14},{14,0},{1,3},{3,5},... | collective-permute-start | bytes 9800 | tf_op jit(solution)/shard_map/ppermute | solution.py:20
  184.8 47.3 %copy-start.2 = (f32[3,8,128]{2,1,0:T(8,128)}, f32[3,8,128]{2,1,0:T(8,128)S(1)}, u32[]{:S(2)}) copy-start(f32[3,8,128]{2,1,0:T(8,128)S(1)} %pad_add_fusion) | copy-start | bytes 36868
  186.2 4.5 %collective-permute-start.18 = (f32[3,8,34]{2,1,0:T(8,128)S(1)}, f32[3,8,34]{2,1,0:T(8,128)S(1)}, u32[]{:S(2)}, u32[]{:S(2)}) collective-permute-start(f32[3,8,34]{2,1,0:T(8,128)S(1)} %pad_maximum_fusion.20), channel_id=1, source_target_pairs={{0,14},{2,0},{4,2},{6,4},{8,6},{10,8},{12,10},{14,12},{1,15},{3,1}... | collective-permute-start | bytes 9800 | tf_op jit(solution)/shard_map/ppermute | solution.py:20
  190.9 4.6 %collective-permute-start.19 = (f32[3,8,153]{2,1,0:T(8,128)S(1)}, f32[3,8,153]{2,1,0:T(8,128)S(1)}, u32[]{:S(2)}, u32[]{:S(2)}) collective-permute-start(f32[3,8,153]{2,1,0:T(8,128)S(1)} %pad_maximum_fusion.6), channel_id=1, source_target_pairs={{0,240},{16,0},{32,16},{48,32},{64,48},{80,64},{96,80},{112,96},{1... | collective-permute-start | bytes 44072 | tf_op jit(solution)/shard_map/ppermute | solution.py:20
  195.7 7.1 %collective-permute-start.20 = (f32[3,8,18]{2,1,0:T(8,128)S(1)}, f32[3,8,18]{2,1,0:T(8,128)S(1)}, u32[]{:S(2)}, u32[]{:S(2)}) collective-permute-start(f32[3,8,18]{2,1,0:T(8,128)S(1)} %pad_maximum_fusion.21), channel_id=1, source_target_pairs={{0,1},{1,0},{2,3},{3,2},{4,5},{5,4},{6,7},{7,6},{8,9},{9,8},{10,11... | collective-permute-start | bytes 5192 | tf_op jit(solution)/shard_map/ppermute | solution.py:20
  208.9 3.1 %collective-permute-start.21 = (f32[3,8,18]{2,1,0:T(8,128)S(1)}, f32[3,8,18]{2,1,0:T(8,128)S(1)}, u32[]{:S(2)}, u32[]{:S(2)}) collective-permute-start(f32[3,8,18]{2,1,0:T(8,128)S(1)} %pad_maximum_fusion.22), channel_id=1, source_target_pairs={{0,1},{1,0},{2,3},{3,2},{4,5},{5,4},{6,7},{7,6},{8,9},{9,8},{10,11... | collective-permute-start | bytes 5192 | tf_op jit(solution)/shard_map/ppermute | solution.py:20
  212.2 6.1 %collective-permute-start.22 = (f32[3,8,153]{2,1,0:T(8,128)S(1)}, f32[3,8,153]{2,1,0:T(8,128)S(1)}, u32[]{:S(2)}, u32[]{:S(2)}) collective-permute-start(f32[3,8,153]{2,1,0:T(8,128)S(1)} %pad_maximum_fusion.7), channel_id=1, source_target_pairs={{0,16},{16,32},{32,48},{48,64},{64,80},{80,96},{96,112},{112,128},... | collective-permute-start | bytes 44072 | tf_op jit(solution)/shard_map/ppermute | solution.py:20
  218.4 6.0 %collective-permute-start.23 = (f32[3,8,34]{2,1,0:T(8,128)S(1)}, f32[3,8,34]{2,1,0:T(8,128)S(1)}, u32[]{:S(2)}, u32[]{:S(2)}) collective-permute-start(f32[3,8,34]{2,1,0:T(8,128)S(1)} %pad_maximum_fusion.23), channel_id=1, source_target_pairs={{0,2},{2,4},{4,6},{6,8},{8,10},{10,12},{12,14},{14,0},{1,3},{3,5},... | collective-permute-start | bytes 9800 | tf_op jit(solution)/shard_map/ppermute | solution.py:20
